TPU v7x, 32 devices: a whole 2x2x4 slice. The times are simulated.
32 devices in a mesh: expert: 8 (over z, y), helper: 4 (over x, core).
Axes of the slice: x: 2, y: 2, z: 4, core: 2. Of those that a mesh axis runs over, the one named last changes fastest.
Arguments:
- tokens: bfloat16 [32768, 768], P(('expert', 'helper')), may hold values from -6 to 6
- gate: float32 [32768], P(('expert', 'helper')), may hold values from 0.2 to 1
- expert_ids: int32 [32768, 1], P(('expert', 'helper')), may hold values from 0 to 31; in each aligned block of 1024 rows (0 to 1023, 1024 to 2047, ...) at most 48 rows name the same one
- backup_ids: int32 [32768, 1], P(('expert', 'helper')), may hold values from 0 to 31; in each aligned block of 1024 rows (0 to 1023, 1024 to 2047, ...) at most 48 rows name the same one
- capacity: int32 [32], replicated, may hold values from 2 to 48
- w_in: bfloat16 [32, 768, 3072], P('expert', None, 'helper'), may hold values from -0.21875 to 0.21875
- w_out: bfloat16 [32, 3072, 768], P('expert', 'helper'), may hold values from -0.109375 to 0.109375
Outputs:
- mixed: bfloat16 [32768, 768], P(('expert', 'helper'))
Inputs may be any that keep to these rules, and one draw needn't show every extreme that they name: `expert_ids`: in the rows of one device no expert is the first expert of more than 48 rows; some expert reaches 48. `backup_ids`: in the rows of one device no expert is the backup of more than 48 rows; some expert reaches 48.
All inputs are finite; a program needn't handle non-finite values.
Results may differ from a plain program's by a relative error of at most 0.0095.
Values may be sent and summed in bfloat16 or wider, within the bound.
A program may use at most 192 MiB of HBM per device.

v0:
```python
import functools

import jax
import jax.numpy as jnp
from jax import lax
from jax.experimental import pallas as pl
from jax.experimental.pallas import tpu as pltpu
from jax.sharding import PartitionSpec as P

MESH = pl.DeviceIdType.MESH
TILE = 16
VMEM_BYTES = 63 * 2**20


def exclusive(index, mask, limit):
    out, bit = 0, 1
    while bit < limit:
        one, two = (index // bit) % 2, (mask // bit) % 2
        out = out + bit * (one + two - 2 * one * two)
        bit *= 2
    return out


def outward(owners):
    steps = [step ^ (step // 2) for step in range(2, owners)]
    return steps + [1]


def homeward(owners):
    ends = sorted(range(owners), key=lambda m: (m // 8, (6, 4, 1, 0)[m // 2 % 4], (m if m // 2 == 3 else -m)))
    middle = sorted(range(owners), key=lambda m: (m // 8, (3, 0, 1, 6)[m // 2 % 4], (m if m // 2 % 4 in (1, 3) else -m)))
    return ends, middle


def windows(held, tiles):
    reach = [min(tiles, -(-(4 * i + 5) * tiles // 13)) for i in range(held // 2)]
    front = [(0, r) for r in reach]
    rear = [(tiles - r, tiles) for r in reach]
    return front + rear[::-1]


def layer_kernel(
    owners, helpers, held, send, wi_hbm, wo_hbm, back, flags, x, o, near, far_in, wi, wo,
    zs, zr, xs, xr, cs, cr, gs, gr, fs, fr, hs, hr, ws, last,
):
    e, h = lax.axis_index("expert"), lax.axis_index("helper")
    hx, hc = exclusive(h, helpers // 2, helpers), exclusive(h, 1, helpers)
    hxc = exclusive(hc, helpers // 2, helpers)
    tiles, width = x.shape[2], x.shape[4]
    f32, bf16 = jnp.float32, jnp.bfloat16

    def partner(k):
        return exclusive(e, k, owners)

    def to_owner(k):
        return pltpu.make_async_remote_copy(
            send.at[partner(k)], x.at[h, e], zs.at[k], zr.at[k], device_id=(partner(k), h), device_id_type=MESH
        )

    def from_owner(k):
        return pltpu.make_async_remote_copy(
            send.at[e], x.at[h, partner(k)], zs.at[k], zr.at[k], device_id=(partner(k), h), device_id_type=MESH
        )

    def across(k):
        return pltpu.make_async_remote_copy(
            x.at[h, partner(k)], x.at[h, partner(k)], xs.at[k], xr.at[k], device_id=(e, hx), device_id_type=MESH
        )

    def from_across(k):
        return pltpu.make_async_remote_copy(
            send.at[e], x.at[hx, partner(k)], xs.at[k], xr.at[k], device_id=(e, hx), device_id_type=MESH
        )

    def beside(k, far):
        block = x.at[hx if far else h, partner(k)]
        return pltpu.make_async_remote_copy(
            block, block, cs.at[far, k], cr.at[far, k], device_id=(e, hc), device_id_type=MESH
        )

    def from_beside(k, far):
        return pltpu.make_async_remote_copy(
            send.at[e], x.at[hxc if far else hc, partner(k)], cs.at[far, k], cr.at[far, k],
            device_id=(e, hc), device_id_type=MESH,
        )

    def give(k, far):
        return pltpu.make_async_remote_copy(
            o.at[hxc if far else hc, partner(k)], near.at[far, k], gs.at[far, k], gr.at[far, k],
            device_id=(e, hc), device_id_type=MESH,
        )

    def pair_over(k):
        return pltpu.make_async_remote_copy(
            o.at[hx, partner(k)], far_in.at[k], fs.at[k], fr.at[k], device_id=(e, hx), device_id_type=MESH
        )

    def home(k):
        return pltpu.make_async_remote_copy(
            o.at[h, partner(k)], back.at[e], hs.at[k], hr.at[k], device_id=(partner(k), h), device_id_type=MESH
        )

    def from_home(k):
        return pltpu.make_async_remote_copy(
            o.at[h, e], back.at[partner(k)], hs.at[k], hr.at[k], device_id=(partner(k), h), device_id_type=MESH
        )

    def weights(j):
        return (
            pltpu.make_async_copy(wi_hbm.at[j], wi.at[j], ws.at[0, j]),
            pltpu.make_async_copy(wo_hbm.at[j], wo.at[j], ws.at[1, j]),
        )

    for j in range(held):
        for copy in weights(j):
            copy.start()
    barrier = pltpu.get_barrier_semaphore()
    for k in range(1, owners):
        pl.semaphore_signal(barrier, inc=1, device_id=(partner(k), h), device_id_type=MESH)
    for other in (hx, hc):
        pl.semaphore_signal(barrier, inc=1, device_id=(e, other), device_id_type=MESH)

    def fill(t, carry):
        x[h, e, t] = send[e, t]
        return carry

    lax.fori_loop(0, tiles, fill, 0)
    pl.semaphore_wait(barrier, owners + 1)
    for k in outward(owners):
        to_owner(k).start()
    across(0).start()
    beside(0, 0).start()

    def clear(i, carry):
        o[i // (owners * tiles), (i // tiles) % owners, i % tiles] = jnp.zeros((TILE, width), bf16)
        return carry

    lax.fori_loop(0, helpers * owners * tiles, clear, 0)
    flags[...] = jnp.zeros(flags.shape, f32)
    for j in range(held):
        for copy in weights(j):
            copy.wait()

    in_middle = exclusive((e // 2) % 2, (e // 4) % 2, 2)
    plan = [(min(one, two), one + in_middle * (two - one)) for one, two in zip(*homeward(owners))]

    def add_pair(k):
        give(k, 1).wait_recv()

        def one_tile(t, carry):
            o[hx, partner(k), t] = (o[hx, partner(k), t].astype(f32) + near[1, k, t].astype(f32)).astype(bf16)
            return carry

        lax.fori_loop(0, tiles, one_tile, 0)

    def add_all(k):
        give(k, 0).wait_recv()
        pair_over(k).wait_recv()

        def one_tile(t, carry):
            o[h, partner(k), t] = (
                o[h, partner(k), t].astype(f32) + near[0, k, t].astype(f32) + far_in[k, t].astype(f32)
            ).astype(bf16)
            return carry

        lax.fori_loop(0, tiles, one_tile, 0)

    def compute(k):
        source = partner(k)
        notes = [x[c, source, tiles - 1][TILE - 1 : TILE, :128].astype(f32) for c in range(helpers)]
        seen = flags[0:1, :]
        for note in notes:
            seen = jnp.maximum(seen, note)
        flags[0:1, :] = seen
        for j, (low, high) in enumerate(windows(held, tiles)):
            size = (high - low) * TILE
            taken = jnp.concatenate([x[c, source, low:high].reshape(size, width) for c in range(helpers)], axis=0)
            hidden = jnp.maximum(jnp.dot(taken, wi[j], preferred_element_type=f32), 0.0).astype(bf16)
            made = jnp.dot(hidden, wo[j], preferred_element_type=f32)
            row = (lax.broadcasted_iota(jnp.int32, (size, width), 0) + low * TILE).astype(f32)
            for c in range(helpers):
                mine = (row >= notes[c][:, j : j + 1]) & (row < notes[c][:, held + j : held + j + 1])
                old = o[c, source, low:high].reshape(size, width).astype(f32)
                new = jnp.where(mine, made[c * size : (c + 1) * size], old).astype(bf16)
                o[c, source, low:high] = new.reshape(high - low, TILE, width)

    early = 2

    def step(i, carry):
        k = exclusive(i, i // 2, owners)

        @pl.when(i + 1 < owners)
        def _():
            ahead = exclusive(i + 1, (i + 1) // 2, owners)
            from_owner(ahead).wait_recv()
            across(ahead).start()
            beside(ahead, 0).start()

        from_across(k).wait_recv()
        beside(k, 1).start()

        @pl.when(i > 0)
        def _():
            before = exclusive(i - 1, (i - 1) // 2, owners)
            give(before, 1).start()
            give(before, 0).start()

        @pl.when(i + 1 == owners)
        def _():
            for _, first in plan[:early]:
                add_pair(first)
            for _, first in plan[:early]:
                pair_over(first).start()

        from_beside(k, 0).wait_recv()
        from_beside(k, 1).wait_recv()
        compute(k)
        return carry

    lax.fori_loop(0, owners, step, 0)
    final = (owners - 1) ^ ((owners - 1) // 2)
    waiting = None
    for n, (_, k) in enumerate(plan[early:]):
        if n == 1:
            give(final, 1).start()
            give(final, 0).start()
        add_pair(k)
        if waiting is not None:
            pair_over(waiting).start()
        waiting = k
    add_all(plan[0][1])
    pair_over(waiting).start()

    def send_home(always, k):
        if always:
            home(k).start()
        else:

            @pl.when(k > 0)
            def _():
                home(k).start()

    waiting = plan[0]
    for always, k in plan[1:]:
        add_all(k)
        send_home(*waiting)
        waiting = always, k
    for k in range(owners):
        across(k).wait_send()
        pair_over(k).wait_send()
        for far in (0, 1):
            beside(k, far).wait_send()
            give(k, far).wait_send()
        if k:
            to_owner(k).wait_send()
    send_home(*waiting)
    mine = pltpu.make_async_copy(o.at[h, e], back.at[e], last)
    mine.start()
    for k in range(1, owners):
        home(k).wait_send()
        from_home(k).wait_recv()
    mine.wait()


def earlier_counts(onehot):
    rows = onehot.shape[0]
    earlier = lax.broadcasted_iota(jnp.int32, (rows, rows), 0) > lax.broadcasted_iota(jnp.int32, (rows, rows), 1)
    return jnp.dot(earlier.astype(jnp.bfloat16), onehot.astype(jnp.bfloat16), preferred_element_type=jnp.float32)


def chosen(onehot, values):
    return jnp.sum(jnp.where(onehot, values, 0.0), axis=1).astype(jnp.int32)


def assign(first, backup, capacity, experts):
    columns = jnp.arange(experts, dtype=jnp.int32)
    room = capacity.astype(jnp.float32)[None, :]
    onehot = first[:, None] == columns[None, :]
    before = earlier_counts(onehot)
    kept = chosen(onehot, room - before) > 0
    spill = (backup[:, None] == columns[None, :]) & ~kept[:, None]
    spilled = earlier_counts(spill)
    kept_count = jnp.minimum(jnp.sum(onehot.astype(jnp.float32), axis=0, keepdims=True), room)
    counts = kept_count + jnp.sum(spill.astype(jnp.float32), axis=0, keepdims=True)
    final = (onehot & kept[:, None]) | spill
    rank = jnp.where(kept[:, None], before, kept_count + spilled)
    return final, rank, counts[0].astype(jnp.int32)


def on_device(tokens, gate, expert_ids, backup_ids, capacity, w_in, w_out):
    held = w_in.shape[0]
    owners, helpers = lax.axis_size("expert"), lax.axis_size("helper")
    rows, width = tokens.shape
    experts = held * owners
    tiles = -(-(13 * rows // (8 * owners)) // TILE)
    block = tiles * TILE
    usable = block - 1
    f32, bf16 = jnp.float32, jnp.bfloat16
    dma = pltpu.SemaphoreType.DMA
    anywhere = pl.BlockSpec(memory_space=pl.ANY)
    vmem = pl.BlockSpec(memory_space=pltpu.VMEM)
    piece = (tiles, TILE, width)

    layer = pl.pallas_call(
        functools.partial(layer_kernel, owners, helpers, held),
        out_shape=(jax.ShapeDtypeStruct((owners,) + piece, bf16), jax.ShapeDtypeStruct((8, 128), f32)),
        in_specs=[vmem, anywhere, anywhere],
        out_specs=(anywhere, vmem),
        scratch_shapes=[
            pltpu.VMEM((helpers, owners) + piece, bf16),
            pltpu.VMEM((helpers, owners) + piece, bf16),
            pltpu.VMEM((2, owners) + piece, bf16),
            pltpu.VMEM((owners,) + piece, bf16),
            pltpu.VMEM(w_in.shape, bf16),
            pltpu.VMEM(w_out.shape, bf16),
            dma((owners,)), dma((owners,)), dma((owners,)), dma((owners,)),
            dma((2, owners)), dma((2, owners)), dma((2, owners)), dma((2, owners)),
            dma((owners,)), dma((owners,)), dma((owners,)), dma((owners,)),
            dma((2, held)), dma,
        ],
        compiler_params=pltpu.CompilerParams(collective_id=0, has_side_effects=True, vmem_limit_bytes=VMEM_BYTES),
        name="layer",
    )

    final, rank, counts = assign(expert_ids[:, 0], backup_ids[:, 0], capacity, experts)
    spans = windows(held, tiles)

    def exchange(done):
        todo = (counts - done).reshape(owners, held)
        takes, starts, used = [None] * held, [None] * held, 0
        for j in range(held // 2):
            takes[j] = jnp.minimum(todo[:, j], spans[j][1] * TILE - used)
            if spans[j][1] == tiles:
                takes[j] = jnp.minimum(takes[j], usable - used)
            starts[j] = used + jnp.zeros_like(takes[j])
            used = used + takes[j]
        end = usable
        for j in range(held - 1, held // 2 - 1, -1):
            takes[j] = jnp.minimum(jnp.minimum(todo[:, j], end - spans[j][0] * TILE), end - used)
            starts[j] = end - takes[j]
            end = end - takes[j]
        takes, starts = jnp.stack(takes, axis=1), jnp.stack(starts, axis=1)
        left = jnp.any(todo > takes)
        offset = rank - done.astype(f32)[None, :]
        flat = takes.reshape(1, experts).astype(f32)
        here = final & (offset >= 0) & (offset < flat)
        base = (starts + jnp.arange(owners, dtype=jnp.int32)[:, None] * block).reshape(1, experts).astype(f32)
        target = jnp.sum(jnp.where(here, offset + base + 1, 0.0), axis=1).astype(jnp.int32) - 1
        hot = lax.broadcasted_iota(jnp.int32, (owners * block, rows), 0) == target[None, :]
        packed = jnp.dot(hot.astype(bf16), tokens, preferred_element_type=f32).reshape(owners, block, width)
        flag = jnp.broadcast_to(left, (owners, 1)).astype(jnp.int32)
        notes = jnp.concatenate([starts, starts + takes, flag], axis=1)
        notes = jnp.pad(notes, ((0, 0), (0, width - 2 * held - 1))).astype(f32)
        is_note = lax.broadcasted_iota(jnp.int32, (owners, block, width), 1) == usable
        packed = jnp.where(is_note, notes[:, None, :], packed).astype(bf16)
        back, flags = layer(packed.reshape((owners,) + piece), w_in, w_out)
        source = target[:, None] == lax.broadcasted_iota(jnp.int32, (rows, owners * block), 1)
        picked = jnp.dot(source.astype(bf16), back.reshape(owners * block, width), preferred_element_type=f32)
        return (gate[:, None] * picked).astype(bf16), target >= 0, done + takes.reshape(experts), flags[0, 2 * held] > 0

    mixed, _, done, more = exchange(jnp.zeros_like(counts))

    def again(state):
        mixed, done, _ = state
        late, here, done, more = exchange(done)
        return jnp.where(here[:, None], late, mixed), done, more

    return lax.while_loop(lambda state: state[2], again, (mixed, done, more))[0]


def solution(mesh):
    placed = (
        P(("expert", "helper"), None),
        P(("expert", "helper")),
        P(("expert", "helper"), None),
        P(("expert", "helper"), None),
        P(),
        P("expert", None, "helper"),
        P("expert", "helper", None),
    )
    return jax.shard_map(
        on_device, mesh=mesh, in_specs=placed, out_specs=P(("expert", "helper"), None), check_vma=False
    )
```

profile of v0, /device:TPU:8, one launch (start us, length us, event | category | flops | bytes accessed | tf_op | source)
XLA Modules:
  0.0 175.9 jit_solution(15030512140678921591)
XLA Ops:
  0.0 0.0 copy-start.2
  0.0 0.8 convert_element_type.184
  0.8 1.4 select_reduce_fusion.2
  2.2 0.8 convert_reduce_fusion
  3.0 0.7 add_convert_fusion.2
  3.7 0.1 convert_element_type.189
  3.8 0.1 subtract_minimum_fusion.3
  3.9 0.1 subtract_minimum_fusion.5
  3.9 0.1 fusion.33
  4.0 0.1 reshape.184
  4.1 0.6 compare_reduce_fusion.1
  5.4 0.1 convert_element_type.192
  5.5 1.3 select_reduce_fusion.1
  6.8 0.1 concatenate.14
  6.9 0.2 copy.9
  7.1 0.0 copy-done.2
  7.1 3.3 %fusion.15 = bf16[1664,768]{1,0:T(8,128)(2,1)S(1)} fusion(bf16[1024,768]{1,0:T(8,128)(2,1)S(1)} %copy-done.2, s32[1024]{0:T(1024)S(1)} %convert_add_fusion.1), kind=kOutput, calls=%fused_computation.38 | convolution fusion | flops 2618949632 | bytes 4132864 | tf_op jit(solution)/shard_map/dot_general | solution.py:350
  10.4 1.7 select_convert_fusion.1.send
  12.2 0.0 copy-start.5
  12.2 155.1 %layer.8 = (bf16[8,13,16,768]{3,2,1,0:T(8,128)(2,1)}, f32[8,128]{1,0:T(8,128)}) custom-call(bf16[8,13,16,768]{3,2,1,0:T(8,128)(2,1)} %select_convert_fusion.1.send, bf16[4,768,768]{2,1,0:T(8,128)(2,1)} %wi_hbm.1, bf16[4,768,768]{2,1,0:T(8,128)(2,1)} %wo_hbm.1), custom_call_target="tpu_custom_call" | custom-call | tf_op jit(solution)/shard_map/layer/pallas_call | solution.py:356
  167.3 1.3 slice.64
  169.2 0.0 copy-done.5
  169.2 0.0 copy-start
  169.3 0.0 copy-start.1
  169.3 0.0 copy-start.3
  169.3 6.3 %multiply_convert_fusion.1 = bf16[1024,768]{1,0:T(8,128)(2,1)} fusion(bf16[1664,768]{1,0:T(8,128)(2,1)} %bitcast.31, s32[1024]{0:T(1024)S(1)} %convert_add_fusion.1, f32[1024]{0:T(1024)S(1)} %copy-done.5), kind=kOutput, calls=%fused_computation.45 | convolution fusion | flops 2620522496 | bytes 4136960 | tf_op jit(solution)/shard_map/dot_general | solution.py:358
  175.6 0.0 copy-done
  175.6 0.0 copy-done.1
  175.6 0.0 copy-done.3
  175.6 0.2 while.17
  (8 shorter events, 0.0 us)
Async XLA Ops:
  0.0 7.1 %copy-start.2 = (bf16[1024,768]{1,0:T(8,128)(2,1)S(1)}, bf16[1024,768]{1,0:T(8,128)(2,1)}, u32[]{:S(2)}) copy-start(bf16[1024,768]{1,0:T(8,128)(2,1)} %param.9) | copy-start | bytes 4718596
  12.2 157.1 %copy-start.5 = (f32[1024]{0:T(1024)S(1)}, f32[1024]{0:T(1024)}, u32[]{:S(2)}) copy-start(f32[1024]{0:T(1024)} %param.10) | copy-start | bytes 12292
  169.2 6.3 %copy-start = (s32[1024,1]{0,1:T(1,128)S(1)}, s32[1024,1]{0,1:T(1,128)}, u32[]{:S(2)}) copy-start(s32[1024,1]{0,1:T(1,128)} %param.12) | copy-start | bytes 12292
  169.3 6.3 %copy-start.1 = (s32[1024,1]{0,1:T(1,128)S(1)}, s32[1024,1]{0,1:T(1,128)}, u32[]{:S(2)}) copy-start(s32[1024,1]{0,1:T(1,128)} %param.11) | copy-start | bytes 12292
  169.3 6.3 %copy-start.3 = (bf16[1024,768]{1,0:T(8,128)(2,1)S(1)}, bf16[1024,768]{1,0:T(8,128)(2,1)}, u32[]{:S(2)}) copy-start(bf16[1024,768]{1,0:T(8,128)(2,1)} %param.9) | copy-start | bytes 4718596
where the time goes:
time: 176 us
  Pallas kernels  155 us (88%)
  matrix products  12.3 us (7%)
  other arithmetic  4.93 us (3%)
  local copies, waits for them, and re-layouts  1.81 us (1%)
    pallas_call x1, Pallas kernels, exchange(): back, flags = layer(packed.reshape((owners,) + piece), w_in, w_out)  155 us
    dot_general x1, matrix products, exchange(): jnp.dot(source.astype(bf16), back.reshape(owners * block, width), preferr...  6.3 us

commit v1 on v0

v1 whole, which is shorter than its diff:
```python
import functools

import jax
import jax.numpy as jnp
from jax import lax
from jax.experimental import pallas as pl
from jax.experimental.pallas import tpu as pltpu
from jax.sharding import PartitionSpec as P

MESH = pl.DeviceIdType.MESH
TILE = 16
VMEM_BYTES = 63 * 2**20
AHEAD = 2
SEND = (1, 3, 2, 6, 7, 5, 4)
TAKE = (0, 1, 3, 2, 6, 7, 5, 4)
RETURN_ENDS = (6, 7, 5, 4, 3, 2, 1, 0)
RETURN_MIDDLE = (6, 7, 2, 3, 5, 4, 1, 0)


def exclusive(index, mask, limit):
    out, bit = 0, 1
    while bit < limit:
        one, two = (index // bit) % 2, (mask // bit) % 2
        out = out + bit * (one + two - 2 * one * two)
        bit *= 2
    return out


def masks(order, owners):
    return [high + low for high in range(0, owners, 8) for low in order if high + low < owners]


def windows(held, tiles):
    reach = [min(tiles, -(-(4 * i + 5) * tiles // 13)) for i in range(held // 2)]
    front = [(0, r) for r in reach]
    rear = [(tiles - r, tiles) for r in reach]
    return front + rear[::-1]


def layer_kernel(
    owners, helpers, held, send, wi_hbm, wo_hbm, back, flags, x, o, near, far_in, wi, wo,
    zs, zr, xs, xr, cs, cr, gs, gr, fs, fr, hs, hr, ws, last,
):
    e, h = lax.axis_index("expert"), lax.axis_index("helper")
    hx, hc = exclusive(h, helpers // 2, helpers), exclusive(h, 1, helpers)
    hxc = exclusive(hc, helpers // 2, helpers)
    tiles, width = x.shape[2], x.shape[4]
    f32, bf16 = jnp.float32, jnp.bfloat16

    in_middle = exclusive((e // 2) % 2, (e // 4) % 2, 2)

    def partner(k):
        return exclusive(e, k, owners)

    def to_owner(k):
        return pltpu.make_async_remote_copy(
            send.at[partner(k)], x.at[h, e], zs.at[k], zr.at[k], device_id=(partner(k), h), device_id_type=MESH
        )

    def from_owner(k):
        return pltpu.make_async_remote_copy(
            send.at[e], x.at[h, partner(k)], zs.at[k], zr.at[k], device_id=(partner(k), h), device_id_type=MESH
        )

    def across(k):
        return pltpu.make_async_remote_copy(
            x.at[h, partner(k)], x.at[h, partner(k)], xs.at[k], xr.at[k], device_id=(e, hx), device_id_type=MESH
        )

    def from_across(k):
        return pltpu.make_async_remote_copy(
            send.at[e], x.at[hx, partner(k)], xs.at[k], xr.at[k], device_id=(e, hx), device_id_type=MESH
        )

    def beside(k, far):
        block = x.at[hx if far else h, partner(k)]
        return pltpu.make_async_remote_copy(
            block, block, cs.at[far, k], cr.at[far, k], device_id=(e, hc), device_id_type=MESH
        )

    def from_beside(k, far):
        return pltpu.make_async_remote_copy(
            send.at[e], x.at[hxc if far else hc, partner(k)], cs.at[far, k], cr.at[far, k],
            device_id=(e, hc), device_id_type=MESH,
        )

    def give(k, far):
        return pltpu.make_async_remote_copy(
            o.at[hxc if far else hc, partner(k)], near.at[far, k], gs.at[far, k], gr.at[far, k],
            device_id=(e, hc), device_id_type=MESH,
        )

    def pair_over(k):
        return pltpu.make_async_remote_copy(
            o.at[hx, partner(k)], far_in.at[k], fs.at[k], fr.at[k], device_id=(e, hx), device_id_type=MESH
        )

    def home(k):
        return pltpu.make_async_remote_copy(
            o.at[h, partner(k)], back.at[e], hs.at[k], hr.at[k], device_id=(partner(k), h), device_id_type=MESH
        )

    def from_home(k):
        return pltpu.make_async_remote_copy(
            o.at[h, e], back.at[partner(k)], hs.at[k], hr.at[k], device_id=(partner(k), h), device_id_type=MESH
        )

    def weights(j):
        return (
            pltpu.make_async_copy(wi_hbm.at[j], wi.at[j], ws.at[0, j]),
            pltpu.make_async_copy(wo_hbm.at[j], wo.at[j], ws.at[1, j]),
        )

    for j in range(held):
        for copy in weights(j):
            copy.start()
    barrier = pltpu.get_barrier_semaphore()
    for k in range(1, owners):
        pl.semaphore_signal(barrier, inc=1, device_id=(partner(k), h), device_id_type=MESH)
    for other in (hx, hc):
        pl.semaphore_signal(barrier, inc=1, device_id=(e, other), device_id_type=MESH)

    def fill(t, carry):
        x[h, e, t] = send[e, t]
        return carry

    lax.fori_loop(0, tiles, fill, 0)
    pl.semaphore_wait(barrier, owners + 1)
    across(0).start()
    beside(0, 0).start()
    for k in masks((0,) + SEND, owners)[1:]:
        to_owner(k).start()

    flags[...] = jnp.zeros(flags.shape, f32)

    plan = [(min(one, two), one + in_middle * (two - one)) for one, two in zip(masks(RETURN_ENDS, owners), masks(RETURN_MIDDLE, owners))]

    def add_pair(k):
        give(k, 1).wait_recv()

        def one_tile(t, carry):
            o[hx, partner(k), t] = (o[hx, partner(k), t].astype(f32) + near[1, k, t].astype(f32)).astype(bf16)
            return carry

        lax.fori_loop(0, tiles, one_tile, 0)

    def add_all(k):
        give(k, 0).wait_recv()
        pair_over(k).wait_recv()

        def one_tile(t, carry):
            o[h, partner(k), t] = (
                o[h, partner(k), t].astype(f32) + near[0, k, t].astype(f32) + far_in[k, t].astype(f32)
            ).astype(bf16)
            return carry

        lax.fori_loop(0, tiles, one_tile, 0)

    def compute(k):
        source = partner(k)
        notes = [x[c, source, tiles - 1][TILE - 1 : TILE, :128].astype(f32) for c in range(helpers)]
        seen = flags[0:1, :]
        for note in notes:
            seen = jnp.maximum(seen, note)
        flags[0:1, :] = seen
        reached = 0
        spans = windows(held, tiles)
        for j in sorted(range(held), key=lambda j: (spans[j][0] - spans[j][1], j)):
            low, high = spans[j]
            size = (high - low) * TILE
            taken = jnp.concatenate([x[c, source, low:high].reshape(size, width) for c in range(helpers)], axis=0)
            hidden = jnp.maximum(jnp.dot(taken, wi[j], preferred_element_type=f32), 0.0).astype(bf16)
            made = jnp.dot(hidden, wo[j], preferred_element_type=f32)
            row = (lax.broadcasted_iota(jnp.int32, (size, width), 0) + low * TILE).astype(f32)
            fresh = max(low, min(reached, high))
            for c in range(helpers):
                mine = (row >= notes[c][:, j : j + 1]) & (row < notes[c][:, held + j : held + j + 1])
                own = made[c * size : (c + 1) * size]
                if fresh > low:
                    upto = (fresh - low) * TILE
                    old = o[c, source, low:fresh].reshape(upto, width).astype(f32)
                    new = jnp.where(mine[:upto], own[:upto], old).astype(bf16)
                    o[c, source, low:fresh] = new.reshape(fresh - low, TILE, width)
                if high > fresh:
                    after = (fresh - low) * TILE
                    new = jnp.where(mine[after:], own[after:], 0.0).astype(bf16)
                    o[c, source, fresh:high] = new.reshape(high - fresh, TILE, width)
            reached = max(reached, high)

    def give_both(k):
        give(k, 1).start()
        give(k, 0).start()

    def start_home(always, k):
        if always:
            home(k).start()
        else:

            @pl.when(k > 0)
            def _():
                home(k).start()

    def send_pairs(turns):
        for n, (_, k) in enumerate(turns):
            add_pair(k)
            if n:
                pair_over(turns[n - 1][1]).start()
        return turns[-1:]

    taken = masks(TAKE, owners)

    def at(i):
        k = 0
        for n, mask in enumerate(taken):
            k = k + mask * jnp.where(i == n, 1, 0)
        return k

    def forward(k):
        from_owner(k).wait_recv()
        across(k).start()
        beside(k, 0).start()

    for k in taken[1:AHEAD]:
        forward(k)
    for j in range(held):
        for copy in weights(j):
            copy.wait()

    def step(i, carry):
        k = at(i)

        @pl.when(i + AHEAD < owners)
        def _():
            forward(at(i + AHEAD))

        from_across(k).wait_recv()
        beside(k, 1).start()

        @pl.when(i > 0)
        def _():
            give_both(at(i - 1))

        for n, turns in ((owners - 2, plan[:1]), (owners - 1, plan[1:3])):

            @pl.when(i == n)
            def _(turns=turns):
                for _, late in send_pairs(turns):
                    pair_over(late).start()

        from_beside(k, 0).wait_recv()
        from_beside(k, 1).wait_recv()
        compute(k)
        return carry

    lax.fori_loop(0, owners, step, 0)
    for k in range(1, owners):
        to_owner(k).wait_send()
    give_both(taken[-1])
    late = send_pairs(plan[3:])
    add_all(plan[0][1])
    pair_over(late[0][1]).start()
    waiting = plan[0]
    for always, k in plan[1:]:
        add_all(k)
        start_home(*waiting)
        waiting = always, k
    for k in range(owners):
        across(k).wait_send()
        pair_over(k).wait_send()
        for far in (0, 1):
            beside(k, far).wait_send()
            give(k, far).wait_send()
    start_home(*waiting)
    mine = pltpu.make_async_copy(o.at[h, e], back.at[e], last)
    mine.start()
    for k in range(1, owners):
        home(k).wait_send()
        from_home(k).wait_recv()
    mine.wait()


def pack_kernel(owners, held, block, spans, first, backup, capacity, done, tokens, send, where, takes_out):
    f32, bf16, i32 = jnp.float32, jnp.bfloat16, jnp.int32
    experts, rows, width, lanes = owners * held, first.shape[1], tokens.shape[1], 128
    usable, tiles = block - 1, block // TILE
    room = capacity[...].astype(f32)
    expert = lax.broadcasted_iota(i32, (experts, rows), 0)
    earlier = (
        lax.broadcasted_iota(i32, (lanes, lanes), 0) < lax.broadcasted_iota(i32, (lanes, lanes), 1)
    ).astype(f32).astype(bf16)

    def ranks(hit):
        pieces = [hit[:, at : at + lanes] for at in range(0, rows, lanes)]
        inner = jnp.dot(jnp.concatenate(pieces, axis=0).astype(bf16), earlier, preferred_element_type=f32)
        total, out = jnp.zeros((experts, 1), f32), []
        for n, piece in enumerate(pieces):
            out.append(inner[n * experts : (n + 1) * experts] + total)
            total = total + jnp.sum(piece, axis=1, keepdims=True)
        return jnp.concatenate(out, axis=1), total

    chosen = jnp.where(expert == first[...], 1.0, 0.0)
    before, named = ranks(chosen)
    kept = jnp.where(before < room, chosen, 0.0)
    stays = jnp.max(kept, axis=0, keepdims=True)
    spill = jnp.where(expert == backup[...], 1.0 - stays, 0.0)
    spilled, extra = ranks(spill)
    kept_count = jnp.minimum(named, room)
    final = kept + spill
    rank = jnp.where(kept > 0.0, before, kept_count + spilled) - done[...]
    todo = jnp.broadcast_to(kept_count + extra - done[...], (experts, lanes))

    turn = lax.broadcasted_iota(i32, (experts, lanes), 0) % held
    same = (
        lax.broadcasted_iota(i32, (experts, experts), 0) // held == lax.broadcasted_iota(i32, (experts, experts), 1) // held
    ).astype(f32).astype(bf16)

    def group_sum(values):
        return jnp.dot(same, values.astype(bf16), preferred_element_type=f32)

    takes, starts = jnp.zeros((experts, lanes), f32), jnp.zeros((experts, lanes), f32)
    used = jnp.zeros((experts, lanes), f32)
    for j in range(held // 2):
        take = jnp.minimum(todo, min(spans[j][1] * TILE, usable) - used)
        takes = jnp.where(turn == j, take, takes)
        starts = jnp.where(turn == j, used, starts)
        used = used + group_sum(jnp.where(turn == j, take, 0.0))
    end = jnp.full((experts, lanes), float(usable), f32)
    for j in range(held - 1, held // 2 - 1, -1):
        take = jnp.minimum(jnp.minimum(todo, end - spans[j][0] * TILE), end - used)
        takes = jnp.where(turn == j, take, takes)
        starts = jnp.where(turn == j, end - take, starts)
        end = end - group_sum(jnp.where(turn == j, take, 0.0))
    takes_out[...] = takes
    left = jnp.max(todo - takes, axis=0, keepdims=True)

    here = jnp.where((rank >= 0.0) & (rank < takes[:, :1]), final, 0.0)
    base = starts[:, :1] + (lax.broadcasted_iota(i32, (experts, 1), 0) // held * block + 1).astype(f32)
    place = jnp.sum(here * (rank + base), axis=0, keepdims=True).astype(i32) - 1
    where[...] = jnp.broadcast_to(place, where.shape)

    lane = lax.broadcasted_iota(i32, (experts, lanes), 1)
    notes = jnp.where(lane == turn, starts, jnp.where(lane == held + turn, starts + takes, 0.0))
    notes = group_sum(notes)
    notes = jnp.where(lane == 2 * held, jnp.where(left > 0.0, 1.0, 0.0), notes)
    last = lax.broadcasted_iota(i32, (block, lanes), 0) == usable
    data = tokens[...]
    for group in range(owners):
        hot = jnp.where(lax.broadcasted_iota(i32, (block, rows), 0) + group * block == place, 1.0, 0.0).astype(bf16)
        packed = jnp.dot(hot, data, preferred_element_type=f32)
        note = jnp.where(last, notes[group * held : group * held + 1, :], packed[:, :lanes])
        packed = jnp.concatenate([note, packed[:, lanes:]], axis=1).astype(bf16)
        send[group] = packed.reshape(tiles, TILE, width)


def pack(owners, held, tiles, first, backup, capacity, done, tokens):
    rows, width = tokens.shape
    experts = owners * held
    return pl.pallas_call(
        functools.partial(pack_kernel, owners, held, tiles * TILE, windows(held, tiles)),
        out_shape=(
            jax.ShapeDtypeStruct((owners, tiles, TILE, width), jnp.bfloat16),
            jax.ShapeDtypeStruct((8, rows), jnp.int32),
            jax.ShapeDtypeStruct((experts, 128), jnp.float32),
        ),
        in_specs=[pl.BlockSpec(memory_space=pltpu.VMEM)] * 5,
        out_specs=[pl.BlockSpec(memory_space=pltpu.VMEM)] * 3,
        compiler_params=pltpu.CompilerParams(vmem_limit_bytes=40 * 2**20),
        name="pack",
    )(first, backup, capacity, done, tokens)


def on_device(tokens, gate, expert_ids, backup_ids, capacity, w_in, w_out):
    held = w_in.shape[0]
    owners, helpers = lax.axis_size("expert"), lax.axis_size("helper")
    rows, width = tokens.shape
    experts = held * owners
    tiles = -(-(13 * rows // (8 * owners)) // TILE)
    block = tiles * TILE
    f32, bf16 = jnp.float32, jnp.bfloat16
    dma = pltpu.SemaphoreType.DMA
    anywhere = pl.BlockSpec(memory_space=pl.ANY)
    vmem = pl.BlockSpec(memory_space=pltpu.VMEM)
    piece = (tiles, TILE, width)

    layer = pl.pallas_call(
        functools.partial(layer_kernel, owners, helpers, held),
        out_shape=(jax.ShapeDtypeStruct((owners,) + piece, bf16), jax.ShapeDtypeStruct((8, 128), f32)),
        in_specs=[vmem, anywhere, anywhere],
        out_specs=(anywhere, vmem),
        scratch_shapes=[
            pltpu.VMEM((helpers, owners) + piece, bf16),
            pltpu.VMEM((helpers, owners) + piece, bf16),
            pltpu.VMEM((2, owners) + piece, bf16),
            pltpu.VMEM((owners,) + piece, bf16),
            pltpu.VMEM(w_in.shape, bf16),
            pltpu.VMEM(w_out.shape, bf16),
            dma((owners,)), dma((owners,)), dma((owners,)), dma((owners,)),
            dma((2, owners)), dma((2, owners)), dma((2, owners)), dma((2, owners)),
            dma((owners,)), dma((owners,)), dma((owners,)), dma((owners,)),
            dma((2, held)), dma,
        ],
        compiler_params=pltpu.CompilerParams(collective_id=0, has_side_effects=True, vmem_limit_bytes=VMEM_BYTES),
        name="layer",
    )

    first, backup = expert_ids.reshape(1, rows), backup_ids.reshape(1, rows)
    room = capacity.reshape(experts, 1)

    def exchange(done):
        send, places, takes = pack(owners, held, tiles, first, backup, room, done, tokens)
        back, flags = layer(send, w_in, w_out)
        target = places[0]
        source = target[:, None] == lax.broadcasted_iota(jnp.int32, (rows, owners * block), 1)
        picked = jnp.dot(source.astype(bf16), back.reshape(owners * block, width), preferred_element_type=f32)
        return (gate[:, None] * picked).astype(bf16), target >= 0, done + takes[:, :1], flags[0, 2 * held] > 0

    mixed, _, done, more = exchange(jnp.zeros((experts, 1), f32))

    def again(state):
        mixed, done, _ = state
        late, here, done, more = exchange(done)
        return jnp.where(here[:, None], late, mixed), done, more

    return lax.while_loop(lambda state: state[2], again, (mixed, done, more))[0]


def solution(mesh):
    placed = (
        P(("expert", "helper"), None),
        P(("expert", "helper")),
        P(("expert", "helper"), None),
        P(("expert", "helper"), None),
        P(),
        P("expert", None, "helper"),
        P("expert", "helper", None),
    )
    return jax.shard_map(
        on_device, mesh=mesh, in_specs=placed, out_specs=P(("expert", "helper"), None), check_vma=False
    )
```

time: 176 us -> 163 us (0.926)
  the two profiles are of different devices: /device:TPU:8 before, /device:TPU:0 now
where the time goes in v1:
time: 163 us
  Pallas kernels  152 us (93%)
  matrix products  6.3 us (4%)
  local copies, waits for them, and re-layouts  3.5 us (2%)
    pallas_call x1, Pallas kernels, exchange(): back, flags = layer(send, w_in, w_out)  147 us
    dot_general x1, matrix products, exchange(): jnp.dot(source.astype(bf16), back.reshape(owners * block, width), preferr...  6.3 us
    pallas_call x1, Pallas kernels, pack(): pl.pallas_call(functools.partial(pack_kernel, owners, held, tiles * TILE,...  5.09 us

profile of v1, /device:TPU:0, one launch (start us, length us, event | category | flops | bytes accessed | tf_op | source)
XLA Modules:
  0.0 162.7 jit_solution(18367327138187318826)
XLA Ops:
  0.0 0.7 copy.8.capacity
  0.7 5.1 %pack.2 = (bf16[8,13,16,768]{3,2,1,0:T(8,128)(2,1)S(1)}, s32[8,1024]{1,0:T(8,128)S(1)}, f32[32,128]{1,0:T(8,128)S(1)}) custom-call(s32[1,1024]{1,0:T(1,128)} %bitcast.19, s32[1,1024]{1,0:T(1,128)} %bitcast.21, s32[32,1]{1,0:T(8,128)S(1)} %copy.8.capacity, f32[32,1]{1,0:T(8,128)S(1)} %broadcast_in_dim.14.done, bf16[1024,768]{1,0:T(8,128)(2,1)} %tokens.1), custom_call_target="tpu_custom_call" | custom-call | tf_op jit(solution)/shard_map/pack/pallas_call | solution.py:358
  5.8 0.0 copy-start.1
  5.8 1.5 copy-done.1
  7.3 0.0 copy-start.6
  7.3 146.8 %layer.2 = (bf16[8,13,16,768]{3,2,1,0:T(8,128)(2,1)}, f32[8,128]{1,0:T(8,128)}) custom-call(bf16[8,13,16,768]{3,2,1,0:T(8,128)(2,1)} %copy-done.1, bf16[4,768,768]{2,1,0:T(8,128)(2,1)} %wi_hbm.1, bf16[4,768,768]{2,1,0:T(8,128)(2,1)} %wo_hbm.1), custom_call_target="tpu_custom_call" | custom-call | tf_op jit(solution)/shard_map/layer/pallas_call | solution.py:411
  154.1 1.3 slice.20
  156.0 0.0 copy-done.6
  156.1 0.0 copy-start.2
  156.1 0.0 copy-start.4
  156.1 0.0 copy-start.5
  156.1 6.3 %multiply_convert_fusion.1 = bf16[1024,768]{1,0:T(8,128)(2,1)} fusion(bf16[1664,768]{1,0:T(8,128)(2,1)} %bitcast.26, s32[1024]{0:T(1024)S(1)} %bitcast.23, f32[1024]{0:T(1024)S(1)} %copy-done.6), kind=kOutput, calls=%fused_computation.10 | convolution fusion | flops 2620522496 | bytes 4136960 | tf_op jit(solution)/shard_map/dot_general | solution.py:414
  162.4 0.0 copy-done.2
  162.4 0.0 copy-done.4
  162.4 0.0 copy-done.5
  162.4 0.2 while.12
  (2 shorter events, 0.0 us)
Async XLA Ops:
  5.8 1.5 copy-start.1
  7.3 148.7 %copy-start.6 = (f32[1024]{0:T(1024)S(1)}, f32[1024]{0:T(1024)}, u32[]{:S(2)}) copy-start(f32[1024]{0:T(1024)} %param.10) | copy-start | bytes 12292
  156.1 6.3 %copy-start.2 = (bf16[1024,768]{1,0:T(8,128)(2,1)S(1)}, bf16[1024,768]{1,0:T(8,128)(2,1)}, u32[]{:S(2)}) copy-start(bf16[1024,768]{1,0:T(8,128)(2,1)} %tokens.1) | copy-start | bytes 4718596
  156.1 6.3 %copy-start.4 = (s32[1024,1]{0,1:T(1,128)S(1)}, s32[1024,1]{0,1:T(1,128)}, u32[]{:S(2)}) copy-start(s32[1024,1]{0,1:T(1,128)} %param.11) | copy-start | bytes 12292
  156.1 6.3 %copy-start.5 = (s32[1024,1]{0,1:T(1,128)S(1)}, s32[1024,1]{0,1:T(1,128)}, u32[]{:S(2)}) copy-start(s32[1024,1]{0,1:T(1,128)} %param.12) | copy-start | bytes 12292

commit v2 on v1

--- a/solution.py
+++ b/solution.py
@@ -38,13 +38,14 @@
 
 
 def layer_kernel(
-    owners, helpers, held, send, wi_hbm, wo_hbm, back, flags, x, o, near, far_in, wi, wo,
-    zs, zr, xs, xr, cs, cr, gs, gr, fs, fr, hs, hr, ws, last,
+    owners, helpers, held, send, places, wi_hbm, wo_hbm, picked, flags, back, x, o, near, far_in, wi, wo,
+    zs, zr, xs, xr, cs, cr, gs, gr, fs, fr, hs, hr, ws,
 ):
     e, h = lax.axis_index("expert"), lax.axis_index("helper")
     hx, hc = exclusive(h, helpers // 2, helpers), exclusive(h, 1, helpers)
     hxc = exclusive(hc, helpers // 2, helpers)
     tiles, width = x.shape[2], x.shape[4]
+    rows, block = places.shape[1], x.shape[2] * TILE
     f32, bf16 = jnp.float32, jnp.bfloat16
 
     in_middle = exclusive((e // 2) % 2, (e // 4) % 2, 2)
@@ -128,10 +129,11 @@
     pl.semaphore_wait(barrier, owners + 1)
     across(0).start()
     beside(0, 0).start()
-    for k in masks((0,) + SEND, owners)[1:]:
+    for k in masks((0,) + tuple(SEND), owners)[1:]:
         to_owner(k).start()
 
     flags[...] = jnp.zeros(flags.shape, f32)
+    picked[...] = jnp.zeros(picked.shape, bf16)
 
     plan = [(min(one, two), one + in_middle * (two - one)) for one, two in zip(masks(RETURN_ENDS, owners), masks(RETURN_MIDDLE, owners))]
 
@@ -264,19 +266,43 @@
         add_all(k)
         start_home(*waiting)
         waiting = always, k
+    start_home(*waiting)
+    place = places[0:1, :]
+
+    def keep(t, carry):
+        back[e, t] = o[h, e, t]
+        return carry
+
+    lax.fori_loop(0, tiles, keep, 0)
+
+    def collect(n, carry):
+        hots, found = [], []
+        for k in (owners - 1 - 2 * n, owners - 2 - 2 * n):
+            group = partner(k)
+
+            @pl.when(k > 0)
+            def _(k=k):
+                from_home(k).wait_recv()
+
+            found.append(back[group].reshape(block, width))
+            row = lax.broadcasted_iota(jnp.int32, (block, rows), 0) + group * block
+            hots.append(jnp.where(row == place, 1.0, 0.0).astype(bf16))
+        part = lax.dot_general(
+            jnp.concatenate(hots, axis=0), jnp.concatenate(found, axis=0), (((0,), (0,)), ((), ())),
+            preferred_element_type=f32,
+        )
+        picked[...] = (picked[...].astype(f32) + part).astype(bf16)
+        return carry
+
+    lax.fori_loop(0, owners // 2, collect, 0)
     for k in range(owners):
         across(k).wait_send()
         pair_over(k).wait_send()
         for far in (0, 1):
             beside(k, far).wait_send()
             give(k, far).wait_send()
-    start_home(*waiting)
-    mine = pltpu.make_async_copy(o.at[h, e], back.at[e], last)
-    mine.start()
-    for k in range(1, owners):
-        home(k).wait_send()
-        from_home(k).wait_recv()
-    mine.wait()
+        if k:
+            home(k).wait_send()
 
 
 def pack_kernel(owners, held, block, spans, first, backup, capacity, done, tokens, send, where, takes_out):
@@ -382,12 +408,15 @@
     vmem = pl.BlockSpec(memory_space=pltpu.VMEM)
     piece = (tiles, TILE, width)
 
+    blocks = owners * piece[0] * piece[1] * width * 2
+    room = blocks * (2 * helpers + 4) + 2 * w_in.size * 2 + rows * width * 2 + 12 * 2**20
     layer = pl.pallas_call(
         functools.partial(layer_kernel, owners, helpers, held),
-        out_shape=(jax.ShapeDtypeStruct((owners,) + piece, bf16), jax.ShapeDtypeStruct((8, 128), f32)),
-        in_specs=[vmem, anywhere, anywhere],
-        out_specs=(anywhere, vmem),
+        out_shape=(jax.ShapeDtypeStruct((rows, width), bf16), jax.ShapeDtypeStruct((8, 128), f32)),
+        in_specs=[vmem, vmem, anywhere, anywhere],
+        out_specs=(vmem, vmem),
         scratch_shapes=[
+            pltpu.VMEM((owners,) + piece, bf16),
             pltpu.VMEM((helpers, owners) + piece, bf16),
             pltpu.VMEM((helpers, owners) + piece, bf16),
             pltpu.VMEM((2, owners) + piece, bf16),
@@ -397,22 +426,22 @@
             dma((owners,)), dma((owners,)), dma((owners,)), dma((owners,)),
             dma((2, owners)), dma((2, owners)), dma((2, owners)), dma((2, owners)),
             dma((owners,)), dma((owners,)), dma((owners,)), dma((owners,)),
-            dma((2, held)), dma,
+            dma((2, held)),
         ],
-        compiler_params=pltpu.CompilerParams(collective_id=0, has_side_effects=True, vmem_limit_bytes=VMEM_BYTES),
+        compiler_params=pltpu.CompilerParams(
+            collective_id=0, has_side_effects=True, vmem_limit_bytes=min(VMEM_BYTES, room)
+        ),
         name="layer",
     )
 
     first, backup = expert_ids.reshape(1, rows), backup_ids.reshape(1, rows)
-    room = capacity.reshape(experts, 1)
+    limits = capacity.reshape(experts, 1)
 
     def exchange(done):
-        send, places, takes = pack(owners, held, tiles, first, backup, room, done, tokens)
-        back, flags = layer(send, w_in, w_out)
-        target = places[0]
-        source = target[:, None] == lax.broadcasted_iota(jnp.int32, (rows, owners * block), 1)
-        picked = jnp.dot(source.astype(bf16), back.reshape(owners * block, width), preferred_element_type=f32)
-        return (gate[:, None] * picked).astype(bf16), target >= 0, done + takes[:, :1], flags[0, 2 * held] > 0
+        send, places, takes = pack(owners, held, tiles, first, backup, limits, done, tokens)
+        picked, flags = layer(send, places, w_in, w_out)
+        mixed = (gate[:, None] * picked.astype(f32)).astype(bf16)
+        return mixed, places[0] >= 0, done + takes[:, :1], flags[0, 2 * held] > 0
 
     mixed, _, done, more = exchange(jnp.zeros((experts, 1), f32))
 

time: 163 us -> 160 us (0.982)
  matrix products: 6.3 us -> 0 us
  Pallas kernels: 152 us -> 155 us
    dot_general x1 -> x0, matrix products: 6.3 us -> none  [exchange(): jnp.dot(source.astype(bf16), back.reshape(owners * block, width), preferr...]
    pallas_call x1, Pallas kernels: 147 us -> 150 us  [exchange(): picked, flags = layer(send, places, w_in, w_out)]
where the time goes in v2:
time: 160 us
  Pallas kernels  155 us (97%)
  local copies, waits for them, and re-layouts  2.97 us (2%)
    pallas_call x1, Pallas kernels, exchange(): picked, flags = layer(send, places, w_in, w_out)  150 us
    pallas_call x1, Pallas kernels, pack(): pl.pallas_call(functools.partial(pack_kernel, owners, held, tiles * TILE,...  5.25 us

profile of v2, /device:TPU:0, one launch (start us, length us, event | category | flops | bytes accessed | tf_op | source)
XLA Modules:
  0.0 160.3 jit_solution(15680135561467630726)
XLA Ops:
  0.0 0.7 copy.8.capacity
  0.7 0.0 slice-start
  0.7 0.0 slice-start.2
  0.7 5.2 %pack.2 = (bf16[8,13,16,768]{3,2,1,0:T(8,128)(2,1)S(1)}, s32[8,1024]{1,0:T(8,128)S(1)}, f32[32,128]{1,0:T(8,128)S(1)}) custom-call(s32[1,1024]{1,0:T(1,128)} %bitcast.12, s32[1,1024]{1,0:T(1,128)} %bitcast.14, s32[32,1]{1,0:T(8,128)S(1)} %copy.8.capacity, f32[32,1]{1,0:T(8,128)S(1)} %broadcast_in_dim.14.done, bf16[1024,768]{1,0:T(8,128)(2,1)} %tokens.1), custom_call_target="tpu_custom_call" | custom-call | tf_op jit(solution)/shard_map/pack/pallas_call | solution.py:384
  6.0 0.0 copy-start.1
  6.0 1.5 copy-done.1
  7.5 0.0 copy-start.5
  7.5 0.0 slice-start.1
  7.5 0.0 slice-start.3
  7.5 149.5 %layer.2 = (bf16[1024,768]{1,0:T(8,128)(2,1)S(1)}, f32[8,128]{1,0:T(8,128)S(1)}) custom-call(bf16[8,13,16,768]{3,2,1,0:T(8,128)(2,1)} %copy-done.1, s32[8,1024]{1,0:T(8,128)S(1)} %get-tuple-element.67.places, bf16[4,768,768]{2,1,0:T(8,128)(2,1)} %wi_hbm.1, bf16[4,768,768]{2,1,0:T(8,128)(2,1)} %wo_hbm.1), custom_call_target="tpu_custom_call" | custom-call | tf_op jit(solution)/shard_map/layer/pallas_call | solution.py:442
  157.1 0.6 slice.16
  158.3 0.0 copy-done.5
  158.3 0.0 copy-start.2
  158.3 0.0 copy-start.3
  158.3 0.0 copy-start.4
  158.3 1.5 multiply_convert_fusion.1
  159.8 0.0 slice-done
  159.8 0.0 slice-done.2
  159.8 0.0 slice-done.1
  159.8 0.0 slice-done.3
  159.8 0.1 copy-done.2
  159.9 0.0 copy-done.3
  159.9 0.0 copy-done.4
  160.0 0.2 while.12
  (3 shorter events, 0.0 us)
Async XLA Ops:
  0.7 159.1 %slice-start = ((s8[4718592]{0:T(1024)(128)(4,1)}), s8[4194304]{0:T(1024)(128)(4,1)S(1)}, s32[]{:S(2)}) async-start(s8[4718592]{0:T(1024)(128)(4,1)} %bitcast.7), calls=%async_computation | async-start | bytes 8388608
  0.7 159.1 %slice-start.2 = ((s8[4718592]{0:T(1024)(128)(4,1)}), s8[4194304]{0:T(1024)(128)(4,1)S(1)}, s32[]{:S(2)}) async-start(s8[4718592]{0:T(1024)(128)(4,1)} %bitcast.9), calls=%async_computation.2 | async-start | bytes 8388608
  6.0 1.5 copy-start.1
  7.5 150.8 %copy-start.5 = (f32[1024]{0:T(1024)S(1)}, f32[1024]{0:T(1024)}, u32[]{:S(2)}) copy-start(f32[1024]{0:T(1024)} %param.10) | copy-start | bytes 12292
  7.5 152.3 %slice-start.1 = ((s8[4718592]{0:T(1024)(128)(4,1)}), s8[524288]{0:T(1024)(128)(4,1)S(1)}, s32[]{:S(2)}) async-start(s8[4718592]{0:T(1024)(128)(4,1)} %bitcast.7), calls=%async_computation.1 | async-start | bytes 1048576
  7.5 152.3 %slice-start.3 = ((s8[4718592]{0:T(1024)(128)(4,1)}), s8[524288]{0:T(1024)(128)(4,1)S(1)}, s32[]{:S(2)}) async-start(s8[4718592]{0:T(1024)(128)(4,1)} %bitcast.9), calls=%async_computation.3 | async-start | bytes 1048576
  158.3 1.6 %copy-start.2 = (bf16[1024,768]{1,0:T(8,128)(2,1)S(1)}, bf16[1024,768]{1,0:T(8,128)(2,1)}, u32[]{:S(2)}) copy-start(bf16[1024,768]{1,0:T(8,128)(2,1)} %tokens.1) | copy-start | bytes 4718596
  158.3 1.6 %copy-start.3 = (s32[1024,1]{0,1:T(1,128)S(1)}, s32[1024,1]{0,1:T(1,128)}, u32[]{:S(2)}) copy-start(s32[1024,1]{0,1:T(1,128)} %param.11) | copy-start | bytes 12292
  158.3 1.6 %copy-start.4 = (s32[1024,1]{0,1:T(1,128)S(1)}, s32[1024,1]{0,1:T(1,128)}, u32[]{:S(2)}) copy-start(s32[1024,1]{0,1:T(1,128)} %param.12) | copy-start | bytes 12292
